TPU v7x, 32 devices: a whole 2x2x4 slice. The times are simulated.
32 devices in a mesh: blk: 16 (over z, y, core), rows: 2 (over x).
Axes of the slice: x: 2, y: 2, z: 4, core: 2. Of those that a mesh axis runs over, the one named last changes fastest.
Arguments:
- columns: float32 [2048, 1280], P('blk', 'rows'), may hold values from -9 to 9
- right_factor: float32 [2048, 512], P('blk', 'rows'), may hold values from -6 to 6
Outputs:
- new_columns: float32 [2048, 1280], P('blk', 'rows')
- new_factor: float32 [2048, 512], P('blk', 'rows')
All inputs are finite; a program needn't handle non-finite values.
Results may differ from a plain program's by a relative error of at most 0.0003.
Values sent between devices are 32-bit elements; how exact they have to be, the bound alone decides.
A program may use at most 64 MiB of HBM per device.

v0:
```python
import jax
import jax.numpy as jnp
from jax import lax
from jax.sharding import PartitionSpec as P

STEPS = 6
HIGHEST_PREC = lax.Precision.HIGHEST


def shifted(block, axis, distance):
    devices = range(lax.axis_size(axis))
    route = [((i - distance) % len(devices), i) for i in devices]
    return lax.ppermute(block, axis, route)


def orth_factor(square):
    lower_factor = jnp.linalg.cholesky(jnp.dot(square.T, square, precision=HIGHEST_PREC))
    return jax.scipy.linalg.solve_triangular(lower_factor, square.T, lower=True).T


def rotation(pair_gram):
    first_turn = orth_factor(pair_gram)
    return orth_factor(jnp.dot(pair_gram, first_turn, precision=HIGHEST_PREC))


def gram_of(upper_rows, lower_rows):
    return lax.dot_general(upper_rows, lower_rows, (((1,), (1,)), ((), ())), precision=HIGHEST_PREC)


def rotate(rotation_matrix, blocks):
    return lax.dot_general(
        rotation_matrix, blocks, (((0,), (0,)), ((), ())), precision=HIGHEST_PREC
    )


def body(columns, right_factor):
    block_width = columns.shape[0] // 2
    stay_gram, moving_gram = lax.psum(
        (
            gram_of(columns[:block_width], columns[:block_width]),
            gram_of(columns[block_width:], columns[block_width:]),
        ),
        "rows",
    )

    def advance_cross(step_index, loop_state):
        column_pair, factor_pair, stay_gram, moving_gram = loop_state
        cross_term = lax.psum(gram_of(column_pair[:block_width], column_pair[block_width:]), "rows")
        upper_half = jnp.concatenate([stay_gram, cross_term], 1)
        lower_half = jnp.concatenate([cross_term.T, moving_gram], 1)
        pair_gram = jnp.concatenate([upper_half, lower_half], 0)
        rotation_matrix = rotation(pair_gram)
        column_pair = rotate(rotation_matrix, column_pair)
        factor_pair = rotate(rotation_matrix, factor_pair)
        rotated_gram = rotate(
            rotation_matrix, jnp.dot(pair_gram, rotation_matrix, precision=HIGHEST_PREC)
        )
        arrived = shifted(
            (
                column_pair[block_width:],
                factor_pair[block_width:],
                rotated_gram[block_width:, block_width:],
            ),
            "blk",
            1,
        )
        return (
            jnp.concatenate([column_pair[:block_width], arrived[0]], 0),
            jnp.concatenate([factor_pair[:block_width], arrived[1]], 0),
            rotated_gram[:block_width, :block_width],
            arrived[2],
        )

    result = lax.fori_loop(0, STEPS, advance_cross, (columns, right_factor, stay_gram, moving_gram))
    return (result[0], result[1])


def solution(mesh):
    return jax.shard_map(
        body,
        mesh=mesh,
        in_specs=(P("blk", "rows"), P("blk", "rows")),
        out_specs=(P("blk", "rows"), P("blk", "rows")),
        check_vma=False,
    )
```

profile of v0, /device:TPU:0, one launch (start us, length us, event | category | flops | bytes accessed | tf_op | source)
XLA Modules:
  0.0 402.2 jit_solution(8088612820644958071)
XLA Ops:
  2.2 10.4 %all-reduce = (f32[64,64]{1,0:T(8,128)S(1)}, f32[64,64]{1,0:T(8,128)S(1)}) all-reduce(f32[64,64]{1,0:T(8,128)S(1)} %fusion.17, f32[64,64]{1,0:T(8,128)S(1)} %fusion.15), channel_id=1, replica_groups=mesh['blk'=16,'rows'=2] {'rows'}, use_global_device_ids=true, to_apply=%region_0.0 | all-reduce | flops 8192 | bytes 65536 | tf_op jit(solution)/shard_map/psum | solution.py:38
  12.7 388.7 %while.16 = (s32[]{:T(128)}, f32[128,640]{1,0:T(8,128)S(1)}, f32[128,256]{1,0:T(8,128)S(1)}, f32[64,64]{1,0:T(8,128)S(1)}, f32[64,64]{1,0:T(8,128)S(1)}, /*index=5*/s32[]{:T(128)}) while((s32[]{:T(128)}, f32[128,640]{1,0:T(8,128)S(1)}, f32[128,256]{1,0:T(8,128)S(1)}, f32[64,64]{1,0:T(8,128)S(1)}, f32[64,64]{1,0:T(8,128)S(1)}, ...), condition=%wide.region_6.9_spmd, body=%wide.region_2.8_spmd.sunk | while | flops 384241920 | bytes 6834369 | solution.py:74
  20.7 11.7 %cholesky.144 = f32[128,128]{1,0:T(8,128)S(1)} custom-call(f32[128,128]{1,0:T(8,128)S(1)} %fusion.103), custom_call_target="Cholesky" | custom-call | tf_op jit(solution)/shard_map/while/body/eval_jaxpr/jit(cholesky)/cholesky | solution.py:17
  33.7 9.8 %custom-call.10 = f32[1,128,128]{1,2,0:T(8,128)S(1)} custom-call(f32[1,128,128]{2,1,0:T(8,128)S(1)} %fusion.105), custom_call_target="InvertDiagBlocksLowerTriangular" | custom-call | tf_op jit(solution)/shard_map/while/body/eval_jaxpr/jit(_solve_triangular)/triangular_solve | solution.py:18
  44.5 11.7 %cholesky.145 = f32[128,128]{1,0:T(8,128)S(1)} custom-call(f32[128,128]{1,0:T(8,128)S(1)} %fusion.109), custom_call_target="Cholesky" | custom-call | tf_op jit(solution)/shard_map/while/body/eval_jaxpr/jit(cholesky)/cholesky | solution.py:17
  57.6 9.8 %custom-call.11 = f32[1,128,128]{1,2,0:T(8,128)S(1)} custom-call(f32[1,128,128]{2,1,0:T(8,128)S(1)} %fusion.110), custom_call_target="InvertDiagBlocksLowerTriangular" | custom-call | tf_op jit(solution)/shard_map/while/body/eval_jaxpr/jit(_solve_triangular)/triangular_solve | solution.py:18
  86.5 11.7 %cholesky.144 = f32[128,128]{1,0:T(8,128)S(1)} custom-call(f32[128,128]{1,0:T(8,128)S(1)} %fusion.103), custom_call_target="Cholesky" | custom-call | tf_op jit(solution)/shard_map/while/body/eval_jaxpr/jit(cholesky)/cholesky | solution.py:17
  99.5 9.8 %custom-call.10 = f32[1,128,128]{1,2,0:T(8,128)S(1)} custom-call(f32[1,128,128]{2,1,0:T(8,128)S(1)} %fusion.105), custom_call_target="InvertDiagBlocksLowerTriangular" | custom-call | tf_op jit(solution)/shard_map/while/body/eval_jaxpr/jit(_solve_triangular)/triangular_solve | solution.py:18
  110.4 11.7 %cholesky.145 = f32[128,128]{1,0:T(8,128)S(1)} custom-call(f32[128,128]{1,0:T(8,128)S(1)} %fusion.109), custom_call_target="Cholesky" | custom-call | tf_op jit(solution)/shard_map/while/body/eval_jaxpr/jit(cholesky)/cholesky | solution.py:17
  123.4 9.8 %custom-call.11 = f32[1,128,128]{1,2,0:T(8,128)S(1)} custom-call(f32[1,128,128]{2,1,0:T(8,128)S(1)} %fusion.110), custom_call_target="InvertDiagBlocksLowerTriangular" | custom-call | tf_op jit(solution)/shard_map/while/body/eval_jaxpr/jit(_solve_triangular)/triangular_solve | solution.py:18
  150.8 11.7 %cholesky.144 = f32[128,128]{1,0:T(8,128)S(1)} custom-call(f32[128,128]{1,0:T(8,128)S(1)} %fusion.103), custom_call_target="Cholesky" | custom-call | tf_op jit(solution)/shard_map/while/body/eval_jaxpr/jit(cholesky)/cholesky | solution.py:17
  163.8 9.8 %custom-call.10 = f32[1,128,128]{1,2,0:T(8,128)S(1)} custom-call(f32[1,128,128]{2,1,0:T(8,128)S(1)} %fusion.105), custom_call_target="InvertDiagBlocksLowerTriangular" | custom-call | tf_op jit(solution)/shard_map/while/body/eval_jaxpr/jit(_solve_triangular)/triangular_solve | solution.py:18
  174.6 11.7 %cholesky.145 = f32[128,128]{1,0:T(8,128)S(1)} custom-call(f32[128,128]{1,0:T(8,128)S(1)} %fusion.109), custom_call_target="Cholesky" | custom-call | tf_op jit(solution)/shard_map/while/body/eval_jaxpr/jit(cholesky)/cholesky | solution.py:17
  187.7 9.8 %custom-call.11 = f32[1,128,128]{1,2,0:T(8,128)S(1)} custom-call(f32[1,128,128]{2,1,0:T(8,128)S(1)} %fusion.110), custom_call_target="InvertDiagBlocksLowerTriangular" | custom-call | tf_op jit(solution)/shard_map/while/body/eval_jaxpr/jit(_solve_triangular)/triangular_solve | solution.py:18
  216.0 11.7 %cholesky.144 = f32[128,128]{1,0:T(8,128)S(1)} custom-call(f32[128,128]{1,0:T(8,128)S(1)} %fusion.103), custom_call_target="Cholesky" | custom-call | tf_op jit(solution)/shard_map/while/body/eval_jaxpr/jit(cholesky)/cholesky | solution.py:17
  229.1 9.8 %custom-call.10 = f32[1,128,128]{1,2,0:T(8,128)S(1)} custom-call(f32[1,128,128]{2,1,0:T(8,128)S(1)} %fusion.105), custom_call_target="InvertDiagBlocksLowerTriangular" | custom-call | tf_op jit(solution)/shard_map/while/body/eval_jaxpr/jit(_solve_triangular)/triangular_solve | solution.py:18
  239.9 11.7 %cholesky.145 = f32[128,128]{1,0:T(8,128)S(1)} custom-call(f32[128,128]{1,0:T(8,128)S(1)} %fusion.109), custom_call_target="Cholesky" | custom-call | tf_op jit(solution)/shard_map/while/body/eval_jaxpr/jit(cholesky)/cholesky | solution.py:17
  252.9 9.8 %custom-call.11 = f32[1,128,128]{1,2,0:T(8,128)S(1)} custom-call(f32[1,128,128]{2,1,0:T(8,128)S(1)} %fusion.110), custom_call_target="InvertDiagBlocksLowerTriangular" | custom-call | tf_op jit(solution)/shard_map/while/body/eval_jaxpr/jit(_solve_triangular)/triangular_solve | solution.py:18
  280.3 11.7 %cholesky.144 = f32[128,128]{1,0:T(8,128)S(1)} custom-call(f32[128,128]{1,0:T(8,128)S(1)} %fusion.103), custom_call_target="Cholesky" | custom-call | tf_op jit(solution)/shard_map/while/body/eval_jaxpr/jit(cholesky)/cholesky | solution.py:17
  293.4 9.8 %custom-call.10 = f32[1,128,128]{1,2,0:T(8,128)S(1)} custom-call(f32[1,128,128]{2,1,0:T(8,128)S(1)} %fusion.105), custom_call_target="InvertDiagBlocksLowerTriangular" | custom-call | tf_op jit(solution)/shard_map/while/body/eval_jaxpr/jit(_solve_triangular)/triangular_solve | solution.py:18
  304.2 11.7 %cholesky.145 = f32[128,128]{1,0:T(8,128)S(1)} custom-call(f32[128,128]{1,0:T(8,128)S(1)} %fusion.109), custom_call_target="Cholesky" | custom-call | tf_op jit(solution)/shard_map/while/body/eval_jaxpr/jit(cholesky)/cholesky | solution.py:17
  317.2 9.8 %custom-call.11 = f32[1,128,128]{1,2,0:T(8,128)S(1)} custom-call(f32[1,128,128]{2,1,0:T(8,128)S(1)} %fusion.110), custom_call_target="InvertDiagBlocksLowerTriangular" | custom-call | tf_op jit(solution)/shard_map/while/body/eval_jaxpr/jit(_solve_triangular)/triangular_solve | solution.py:18
  345.5 11.7 %cholesky.144 = f32[128,128]{1,0:T(8,128)S(1)} custom-call(f32[128,128]{1,0:T(8,128)S(1)} %fusion.103), custom_call_target="Cholesky" | custom-call | tf_op jit(solution)/shard_map/while/body/eval_jaxpr/jit(cholesky)/cholesky | solution.py:17
  369.4 11.7 %cholesky.145 = f32[128,128]{1,0:T(8,128)S(1)} custom-call(f32[128,128]{1,0:T(8,128)S(1)} %fusion.109), custom_call_target="Cholesky" | custom-call | tf_op jit(solution)/shard_map/while/body/eval_jaxpr/jit(cholesky)/cholesky | solution.py:17
  (227 shorter events, 151.3 us)
Async XLA Ops:
  1.9 10.8 %copy-start.2 = (f32[128,256]{1,0:T(8,128)S(1)}, f32[128,256]{1,0:T(8,128)}, u32[]{:S(2)}) copy-start(f32[128,256]{1,0:T(8,128)} %param.8) | copy-start | bytes 393220
  68.0 6.4 %collective-permute-start.1 = (f32[64,256]{1,0:T(8,128)S(1)}, f32[64,256]{1,0:T(8,128)S(1)}, u32[]{:S(2)}, u32[]{:S(2)}) collective-permute-start(f32[64,256]{1,0:T(8,128)S(1)} %get-tuple-element.91), channel_id=1, source_target_pairs={{30,0},{0,2},{2,4},{4,6},{6,8},{8,10},{10,12},{12,14},{14,16},{16,... | collective-permute-start | bytes 196616 | tf_op jit(solution)/shard_map/while/body/eval_jaxpr/ppermute | solution.py:13
  68.5 7.7 %collective-permute-start = (f32[64,640]{1,0:T(8,128)S(1)}, f32[64,640]{1,0:T(8,128)S(1)}, u32[]{:S(2)}, u32[]{:S(2)}) collective-permute-start(f32[64,640]{1,0:T(8,128)S(1)} %get-tuple-element.89), channel_id=1, source_target_pairs={{30,0},{0,2},{2,4},{4,6},{6,8},{8,10},{10,12},{12,14},{14,16},{16,... | collective-permute-start | bytes 491528 | tf_op jit(solution)/shard_map/while/body/eval_jaxpr/ppermute | solution.py:13
  71.1 6.0 %collective-permute-start.2 = (f32[64,64]{1,0:T(8,128)S(1)}, f32[64,64]{1,0:T(8,128)S(1)}, u32[]{:S(2)}, u32[]{:S(2)}) collective-permute-start(f32[64,64]{1,0:T(8,128)S(1)} %get-tuple-element.94), channel_id=1, source_target_pairs={{30,0},{0,2},{2,4},{4,6},{6,8},{8,10},{10,12},{12,14},{14,16},{16,... | collective-permute-start | bytes 49160 | tf_op jit(solution)/shard_map/while/body/eval_jaxpr/ppermute | solution.py:13
  133.8 6.4 %collective-permute-start.1 = (f32[64,256]{1,0:T(8,128)S(1)}, f32[64,256]{1,0:T(8,128)S(1)}, u32[]{:S(2)}, u32[]{:S(2)}) collective-permute-start(f32[64,256]{1,0:T(8,128)S(1)} %get-tuple-element.91), channel_id=1, source_target_pairs={{30,0},{0,2},{2,4},{4,6},{6,8},{8,10},{10,12},{12,14},{14,16},{16,... | collective-permute-start | bytes 196616 | tf_op jit(solution)/shard_map/while/body/eval_jaxpr/ppermute | solution.py:13
  134.3 7.7 %collective-permute-start = (f32[64,640]{1,0:T(8,128)S(1)}, f32[64,640]{1,0:T(8,128)S(1)}, u32[]{:S(2)}, u32[]{:S(2)}) collective-permute-start(f32[64,640]{1,0:T(8,128)S(1)} %get-tuple-element.89), channel_id=1, source_target_pairs={{30,0},{0,2},{2,4},{4,6},{6,8},{8,10},{10,12},{12,14},{14,16},{16,... | collective-permute-start | bytes 491528 | tf_op jit(solution)/shard_map/while/body/eval_jaxpr/ppermute | solution.py:13
  135.0 7.4 %collective-permute-start.2 = (f32[64,64]{1,0:T(8,128)S(1)}, f32[64,64]{1,0:T(8,128)S(1)}, u32[]{:S(2)}, u32[]{:S(2)}) collective-permute-start(f32[64,64]{1,0:T(8,128)S(1)} %get-tuple-element.94), channel_id=1, source_target_pairs={{30,0},{0,2},{2,4},{4,6},{6,8},{8,10},{10,12},{12,14},{14,16},{16,... | collective-permute-start | bytes 49160 | tf_op jit(solution)/shard_map/while/body/eval_jaxpr/ppermute | solution.py:13
  198.1 6.4 %collective-permute-start.1 = (f32[64,256]{1,0:T(8,128)S(1)}, f32[64,256]{1,0:T(8,128)S(1)}, u32[]{:S(2)}, u32[]{:S(2)}) collective-permute-start(f32[64,256]{1,0:T(8,128)S(1)} %get-tuple-element.91), channel_id=1, source_target_pairs={{30,0},{0,2},{2,4},{4,6},{6,8},{8,10},{10,12},{12,14},{14,16},{16,... | collective-permute-start | bytes 196616 | tf_op jit(solution)/shard_map/while/body/eval_jaxpr/ppermute | solution.py:13
  198.6 7.7 %collective-permute-start = (f32[64,640]{1,0:T(8,128)S(1)}, f32[64,640]{1,0:T(8,128)S(1)}, u32[]{:S(2)}, u32[]{:S(2)}) collective-permute-start(f32[64,640]{1,0:T(8,128)S(1)} %get-tuple-element.89), channel_id=1, source_target_pairs={{30,0},{0,2},{2,4},{4,6},{6,8},{8,10},{10,12},{12,14},{14,16},{16,... | collective-permute-start | bytes 491528 | tf_op jit(solution)/shard_map/while/body/eval_jaxpr/ppermute | solution.py:13
  199.2 7.4 %collective-permute-start.2 = (f32[64,64]{1,0:T(8,128)S(1)}, f32[64,64]{1,0:T(8,128)S(1)}, u32[]{:S(2)}, u32[]{:S(2)}) collective-permute-start(f32[64,64]{1,0:T(8,128)S(1)} %get-tuple-element.94), channel_id=1, source_target_pairs={{30,0},{0,2},{2,4},{4,6},{6,8},{8,10},{10,12},{12,14},{14,16},{16,... | collective-permute-start | bytes 49160 | tf_op jit(solution)/shard_map/while/body/eval_jaxpr/ppermute | solution.py:13
  263.3 6.4 %collective-permute-start.1 = (f32[64,256]{1,0:T(8,128)S(1)}, f32[64,256]{1,0:T(8,128)S(1)}, u32[]{:S(2)}, u32[]{:S(2)}) collective-permute-start(f32[64,256]{1,0:T(8,128)S(1)} %get-tuple-element.91), channel_id=1, source_target_pairs={{30,0},{0,2},{2,4},{4,6},{6,8},{8,10},{10,12},{12,14},{14,16},{16,... | collective-permute-start | bytes 196616 | tf_op jit(solution)/shard_map/while/body/eval_jaxpr/ppermute | solution.py:13
  263.8 7.7 %collective-permute-start = (f32[64,640]{1,0:T(8,128)S(1)}, f32[64,640]{1,0:T(8,128)S(1)}, u32[]{:S(2)}, u32[]{:S(2)}) collective-permute-start(f32[64,640]{1,0:T(8,128)S(1)} %get-tuple-element.89), channel_id=1, source_target_pairs={{30,0},{0,2},{2,4},{4,6},{6,8},{8,10},{10,12},{12,14},{14,16},{16,... | collective-permute-start | bytes 491528 | tf_op jit(solution)/shard_map/while/body/eval_jaxpr/ppermute | solution.py:13
  264.5 7.4 %collective-permute-start.2 = (f32[64,64]{1,0:T(8,128)S(1)}, f32[64,64]{1,0:T(8,128)S(1)}, u32[]{:S(2)}, u32[]{:S(2)}) collective-permute-start(f32[64,64]{1,0:T(8,128)S(1)} %get-tuple-element.94), channel_id=1, source_target_pairs={{30,0},{0,2},{2,4},{4,6},{6,8},{8,10},{10,12},{12,14},{14,16},{16,... | collective-permute-start | bytes 49160 | tf_op jit(solution)/shard_map/while/body/eval_jaxpr/ppermute | solution.py:13
  327.6 6.4 %collective-permute-start.1 = (f32[64,256]{1,0:T(8,128)S(1)}, f32[64,256]{1,0:T(8,128)S(1)}, u32[]{:S(2)}, u32[]{:S(2)}) collective-permute-start(f32[64,256]{1,0:T(8,128)S(1)} %get-tuple-element.91), channel_id=1, source_target_pairs={{30,0},{0,2},{2,4},{4,6},{6,8},{8,10},{10,12},{12,14},{14,16},{16,... | collective-permute-start | bytes 196616 | tf_op jit(solution)/shard_map/while/body/eval_jaxpr/ppermute | solution.py:13
  328.1 7.7 %collective-permute-start = (f32[64,640]{1,0:T(8,128)S(1)}, f32[64,640]{1,0:T(8,128)S(1)}, u32[]{:S(2)}, u32[]{:S(2)}) collective-permute-start(f32[64,640]{1,0:T(8,128)S(1)} %get-tuple-element.89), channel_id=1, source_target_pairs={{30,0},{0,2},{2,4},{4,6},{6,8},{8,10},{10,12},{12,14},{14,16},{16,... | collective-permute-start | bytes 491528 | tf_op jit(solution)/shard_map/while/body/eval_jaxpr/ppermute | solution.py:13
  328.8 7.4 %collective-permute-start.2 = (f32[64,64]{1,0:T(8,128)S(1)}, f32[64,64]{1,0:T(8,128)S(1)}, u32[]{:S(2)}, u32[]{:S(2)}) collective-permute-start(f32[64,64]{1,0:T(8,128)S(1)} %get-tuple-element.94), channel_id=1, source_target_pairs={{30,0},{0,2},{2,4},{4,6},{6,8},{8,10},{10,12},{12,14},{14,16},{16,... | collective-permute-start | bytes 49160 | tf_op jit(solution)/shard_map/while/body/eval_jaxpr/ppermute | solution.py:13
  392.8 6.4 %collective-permute-start.1 = (f32[64,256]{1,0:T(8,128)S(1)}, f32[64,256]{1,0:T(8,128)S(1)}, u32[]{:S(2)}, u32[]{:S(2)}) collective-permute-start(f32[64,256]{1,0:T(8,128)S(1)} %get-tuple-element.91), channel_id=1, source_target_pairs={{30,0},{0,2},{2,4},{4,6},{6,8},{8,10},{10,12},{12,14},{14,16},{16,... | collective-permute-start | bytes 196616 | tf_op jit(solution)/shard_map/while/body/eval_jaxpr/ppermute | solution.py:13
  393.4 7.7 %collective-permute-start = (f32[64,640]{1,0:T(8,128)S(1)}, f32[64,640]{1,0:T(8,128)S(1)}, u32[]{:S(2)}, u32[]{:S(2)}) collective-permute-start(f32[64,640]{1,0:T(8,128)S(1)} %get-tuple-element.89), channel_id=1, source_target_pairs={{30,0},{0,2},{2,4},{4,6},{6,8},{8,10},{10,12},{12,14},{14,16},{16,... | collective-permute-start | bytes 491528 | tf_op jit(solution)/shard_map/while/body/eval_jaxpr/ppermute | solution.py:13
  394.0 7.4 %collective-permute-start.2 = (f32[64,64]{1,0:T(8,128)S(1)}, f32[64,64]{1,0:T(8,128)S(1)}, u32[]{:S(2)}, u32[]{:S(2)}) collective-permute-start(f32[64,64]{1,0:T(8,128)S(1)} %get-tuple-element.94), channel_id=1, source_target_pairs={{30,0},{0,2},{2,4},{4,6},{6,8},{8,10},{10,12},{12,14},{14,16},{16,... | collective-permute-start | bytes 49160 | tf_op jit(solution)/shard_map/while/body/eval_jaxpr/ppermute | solution.py:13
  401.4 0.7 copy-start
  401.4 0.8 copy-start.1
where the time goes:
time: 403 us; the launch traced here: 402 us
  other arithmetic  275 us (68%)
  blocking collectives  57.1 us (14%)
  waiting for transfers between devices  42.6 us (11%)
  matrix products  17.9 us (4%)
  local copies, waits for them, and re-layouts  4.83 us (1%)
    another operation x36, other arithmetic, orth_factor(): jnp.linalg.cholesky(jnp.dot(square.T, square, precision=HIGHEST_PREC))  149 us
    another operation x24, other arithmetic, orth_factor(): jax.scipy.linalg.solve_triangular(lower_factor, square.T, lower=True)  126 us
    psum x6, blocking collectives, advance_cross(): lax.psum(gram_of(column_pair[:block_width], column_pair[block_width:]), '...  46.7 us
    ppermute x18, waiting for transfers between devices, shifted(): return lax.ppermute(block, axis, route)  42.6 us
    psum x1, blocking collectives, body(): lax.psum((gram_of(columns[:block_width], columns[:block_width]), gram_of(...  10.4 us
  transfers between devices with their start and end apart: 18, of which 18 were waited for; matrix products, arithmetic and copies ran while one was open for 2% of the time, Pallas kernels for 0%

commit v1 on v0

--- a/solution.py
+++ b/solution.py
@@ -5,6 +5,12 @@
 
 STEPS = 6
 HIGHEST_PREC = lax.Precision.HIGHEST
+
+
+def gather_and_add(x, axis):
+    blocks = lax.all_gather(x, axis, axis=0, tiled=False)
+    total = blocks.sum(axis=0)
+    return total
 
 
 def shifted(block, axis, distance):
@@ -45,7 +51,9 @@
 
     def advance_cross(step_index, loop_state):
         column_pair, factor_pair, stay_gram, moving_gram = loop_state
-        cross_term = lax.psum(gram_of(column_pair[:block_width], column_pair[block_width:]), "rows")
+        cross_term = gather_and_add(
+            gram_of(column_pair[:block_width], column_pair[block_width:]), "rows"
+        )
         upper_half = jnp.concatenate([stay_gram, cross_term], 1)
         lower_half = jnp.concatenate([cross_term.T, moving_gram], 1)
         pair_gram = jnp.concatenate([upper_half, lower_half], 0)

time: 403 us -> 382 us (0.948)
  blocking collectives: 57.1 us -> 37.9 us
    psum x6 -> x0, blocking collectives: 46.7 us -> none  [advance_cross(): lax.psum(gram_of(column_pair[:block_width], column_pair[block_width:]), '...]
    all_gather x0 -> x6, blocking collectives: none -> 27.5 us  [gather_and_add(): blocks = lax.all_gather(x, axis, axis=0, tiled=False)]
where the time goes in v1:
time: 382 us; the launch traced here: 381 us
  other arithmetic  275 us (72%)
  waiting for transfers between devices  42.7 us (11%)
  blocking collectives  37.9 us (10%)
  matrix products  17.8 us (5%)
  local copies, waits for them, and re-layouts  3.9 us (1%)
    another operation x36, other arithmetic, orth_factor(): jnp.linalg.cholesky(jnp.dot(square.T, square, precision=HIGHEST_PREC))  149 us
    another operation x24, other arithmetic, orth_factor(): jax.scipy.linalg.solve_triangular(lower_factor, square.T, lower=True)  126 us
    ppermute x18, waiting for transfers between devices, shifted(): return lax.ppermute(block, axis, route)  42.7 us
    all_gather x6, blocking collectives, gather_and_add(): blocks = lax.all_gather(x, axis, axis=0, tiled=False)  27.5 us
    psum x1, blocking collectives, body(): lax.psum((gram_of(columns[:block_width], columns[:block_width]), gram_of(...  10.4 us
  transfers between devices with their start and end apart: 18, of which 18 were waited for; matrix products, arithmetic and copies ran while one was open for 2% of the time, Pallas kernels for 0%

profile of v1, /device:TPU:0, one launch (start us, length us, event | category | flops | bytes accessed | tf_op | source)
XLA Modules:
  0.0 381.5 jit_solution(16539425070175047870)
XLA Ops:
  2.2 10.4 %all-reduce = (f32[64,64]{1,0:T(8,128)S(1)}, f32[64,64]{1,0:T(8,128)S(1)}) all-reduce(f32[64,64]{1,0:T(8,128)S(1)} %fusion.17, f32[64,64]{1,0:T(8,128)S(1)} %fusion.15), channel_id=1, replica_groups=mesh['blk'=16,'rows'=2] {'rows'}, use_global_device_ids=true, to_apply=%region_0.0 | all-reduce | flops 8192 | bytes 65536 | tf_op jit(solution)/shard_map/psum | solution.py:44
  12.7 368.1 %while.16 = (s32[]{:T(128)}, f32[128,640]{1,0:T(8,128)S(1)}, f32[128,256]{1,0:T(8,128)S(1)}, f32[64,64]{1,0:T(8,128)S(1)}, f32[64,64]{1,0:T(8,128)S(1)}, /*index=5*/s32[]{:T(128)}, f32[]{:T(128)}) while((s32[]{:T(128)}, f32[128,640]{1,0:T(8,128)S(1)}, f32[128,256]{1,0:T(8,128)S(1)}, f32[64,64]{1,0:T(8,128)S(1)}, f32[64,64]{1,0:T(8,128)S(1)}, ...), condition=%wide.region_6.9_spmd, body=%wide.region_2.8_spmd.sunk | while | flops 384241920 | bytes 6834381 | solution.py:82
  18.2 11.7 %cholesky.144 = f32[128,128]{1,0:T(8,128)S(1)} custom-call(f32[128,128]{1,0:T(8,128)S(1)} %fusion.103), custom_call_target="Cholesky" | custom-call | tf_op jit(solution)/shard_map/while/body/eval_jaxpr/jit(cholesky)/cholesky | solution.py:23
  31.2 9.8 %custom-call.10 = f32[1,128,128]{1,2,0:T(8,128)S(1)} custom-call(f32[1,128,128]{2,1,0:T(8,128)S(1)} %fusion.105), custom_call_target="InvertDiagBlocksLowerTriangular" | custom-call | tf_op jit(solution)/shard_map/while/body/eval_jaxpr/jit(_solve_triangular)/triangular_solve | solution.py:24
  42.0 11.7 %cholesky.145 = f32[128,128]{1,0:T(8,128)S(1)} custom-call(f32[128,128]{1,0:T(8,128)S(1)} %fusion.109), custom_call_target="Cholesky" | custom-call | tf_op jit(solution)/shard_map/while/body/eval_jaxpr/jit(cholesky)/cholesky | solution.py:23
  55.1 9.8 %custom-call.11 = f32[1,128,128]{1,2,0:T(8,128)S(1)} custom-call(f32[1,128,128]{2,1,0:T(8,128)S(1)} %fusion.110), custom_call_target="InvertDiagBlocksLowerTriangular" | custom-call | tf_op jit(solution)/shard_map/while/body/eval_jaxpr/jit(_solve_triangular)/triangular_solve | solution.py:24
  79.6 11.7 %cholesky.144 = f32[128,128]{1,0:T(8,128)S(1)} custom-call(f32[128,128]{1,0:T(8,128)S(1)} %fusion.103), custom_call_target="Cholesky" | custom-call | tf_op jit(solution)/shard_map/while/body/eval_jaxpr/jit(cholesky)/cholesky | solution.py:23
  92.7 9.8 %custom-call.10 = f32[1,128,128]{1,2,0:T(8,128)S(1)} custom-call(f32[1,128,128]{2,1,0:T(8,128)S(1)} %fusion.105), custom_call_target="InvertDiagBlocksLowerTriangular" | custom-call | tf_op jit(solution)/shard_map/while/body/eval_jaxpr/jit(_solve_triangular)/triangular_solve | solution.py:24
  103.4 11.7 %cholesky.145 = f32[128,128]{1,0:T(8,128)S(1)} custom-call(f32[128,128]{1,0:T(8,128)S(1)} %fusion.109), custom_call_target="Cholesky" | custom-call | tf_op jit(solution)/shard_map/while/body/eval_jaxpr/jit(cholesky)/cholesky | solution.py:23
  116.5 9.8 %custom-call.11 = f32[1,128,128]{1,2,0:T(8,128)S(1)} custom-call(f32[1,128,128]{2,1,0:T(8,128)S(1)} %fusion.110), custom_call_target="InvertDiagBlocksLowerTriangular" | custom-call | tf_op jit(solution)/shard_map/while/body/eval_jaxpr/jit(_solve_triangular)/triangular_solve | solution.py:24
  140.9 11.7 %cholesky.144 = f32[128,128]{1,0:T(8,128)S(1)} custom-call(f32[128,128]{1,0:T(8,128)S(1)} %fusion.103), custom_call_target="Cholesky" | custom-call | tf_op jit(solution)/shard_map/while/body/eval_jaxpr/jit(cholesky)/cholesky | solution.py:23
  154.0 9.8 %custom-call.10 = f32[1,128,128]{1,2,0:T(8,128)S(1)} custom-call(f32[1,128,128]{2,1,0:T(8,128)S(1)} %fusion.105), custom_call_target="InvertDiagBlocksLowerTriangular" | custom-call | tf_op jit(solution)/shard_map/while/body/eval_jaxpr/jit(_solve_triangular)/triangular_solve | solution.py:24
  164.8 11.7 %cholesky.145 = f32[128,128]{1,0:T(8,128)S(1)} custom-call(f32[128,128]{1,0:T(8,128)S(1)} %fusion.109), custom_call_target="Cholesky" | custom-call | tf_op jit(solution)/shard_map/while/body/eval_jaxpr/jit(cholesky)/cholesky | solution.py:23
  177.8 9.8 %custom-call.11 = f32[1,128,128]{1,2,0:T(8,128)S(1)} custom-call(f32[1,128,128]{2,1,0:T(8,128)S(1)} %fusion.110), custom_call_target="InvertDiagBlocksLowerTriangular" | custom-call | tf_op jit(solution)/shard_map/while/body/eval_jaxpr/jit(_solve_triangular)/triangular_solve | solution.py:24
  202.3 11.7 %cholesky.144 = f32[128,128]{1,0:T(8,128)S(1)} custom-call(f32[128,128]{1,0:T(8,128)S(1)} %fusion.103), custom_call_target="Cholesky" | custom-call | tf_op jit(solution)/shard_map/while/body/eval_jaxpr/jit(cholesky)/cholesky | solution.py:23
  215.3 9.8 %custom-call.10 = f32[1,128,128]{1,2,0:T(8,128)S(1)} custom-call(f32[1,128,128]{2,1,0:T(8,128)S(1)} %fusion.105), custom_call_target="InvertDiagBlocksLowerTriangular" | custom-call | tf_op jit(solution)/shard_map/while/body/eval_jaxpr/jit(_solve_triangular)/triangular_solve | solution.py:24
  226.1 11.7 %cholesky.145 = f32[128,128]{1,0:T(8,128)S(1)} custom-call(f32[128,128]{1,0:T(8,128)S(1)} %fusion.109), custom_call_target="Cholesky" | custom-call | tf_op jit(solution)/shard_map/while/body/eval_jaxpr/jit(cholesky)/cholesky | solution.py:23
  239.1 9.8 %custom-call.11 = f32[1,128,128]{1,2,0:T(8,128)S(1)} custom-call(f32[1,128,128]{2,1,0:T(8,128)S(1)} %fusion.110), custom_call_target="InvertDiagBlocksLowerTriangular" | custom-call | tf_op jit(solution)/shard_map/while/body/eval_jaxpr/jit(_solve_triangular)/triangular_solve | solution.py:24
  263.6 11.7 %cholesky.144 = f32[128,128]{1,0:T(8,128)S(1)} custom-call(f32[128,128]{1,0:T(8,128)S(1)} %fusion.103), custom_call_target="Cholesky" | custom-call | tf_op jit(solution)/shard_map/while/body/eval_jaxpr/jit(cholesky)/cholesky | solution.py:23
  276.6 9.8 %custom-call.10 = f32[1,128,128]{1,2,0:T(8,128)S(1)} custom-call(f32[1,128,128]{2,1,0:T(8,128)S(1)} %fusion.105), custom_call_target="InvertDiagBlocksLowerTriangular" | custom-call | tf_op jit(solution)/shard_map/while/body/eval_jaxpr/jit(_solve_triangular)/triangular_solve | solution.py:24
  287.4 11.7 %cholesky.145 = f32[128,128]{1,0:T(8,128)S(1)} custom-call(f32[128,128]{1,0:T(8,128)S(1)} %fusion.109), custom_call_target="Cholesky" | custom-call | tf_op jit(solution)/shard_map/while/body/eval_jaxpr/jit(cholesky)/cholesky | solution.py:23
  324.9 11.7 %cholesky.144 = f32[128,128]{1,0:T(8,128)S(1)} custom-call(f32[128,128]{1,0:T(8,128)S(1)} %fusion.103), custom_call_target="Cholesky" | custom-call | tf_op jit(solution)/shard_map/while/body/eval_jaxpr/jit(cholesky)/cholesky | solution.py:23
  348.7 11.7 %cholesky.145 = f32[128,128]{1,0:T(8,128)S(1)} custom-call(f32[128,128]{1,0:T(8,128)S(1)} %fusion.109), custom_call_target="Cholesky" | custom-call | tf_op jit(solution)/shard_map/while/body/eval_jaxpr/jit(cholesky)/cholesky | solution.py:23
  361.8 9.8 %custom-call.11 = f32[1,128,128]{1,2,0:T(8,128)S(1)} custom-call(f32[1,128,128]{2,1,0:T(8,128)S(1)} %fusion.110), custom_call_target="InvertDiagBlocksLowerTriangular" | custom-call | tf_op jit(solution)/shard_map/while/body/eval_jaxpr/jit(_solve_triangular)/triangular_solve | solution.py:24
  (221 shorter events, 130.7 us)
Async XLA Ops:
  1.9 10.8 %copy-start.2 = (f32[128,256]{1,0:T(8,128)S(1)}, f32[128,256]{1,0:T(8,128)}, u32[]{:S(2)}) copy-start(f32[128,256]{1,0:T(8,128)} %param.8) | copy-start | bytes 393220
  65.5 6.4 %collective-permute-start.1 = (f32[64,256]{1,0:T(8,128)S(1)}, f32[64,256]{1,0:T(8,128)S(1)}, u32[]{:S(2)}, u32[]{:S(2)}) collective-permute-start(f32[64,256]{1,0:T(8,128)S(1)} %get-tuple-element.91), channel_id=1, source_target_pairs={{30,0},{0,2},{2,4},{4,6},{6,8},{8,10},{10,12},{12,14},{14,16},{16,... | collective-permute-start | bytes 196616 | tf_op jit(solution)/shard_map/while/body/eval_jaxpr/ppermute | solution.py:19
  66.0 7.7 %collective-permute-start = (f32[64,640]{1,0:T(8,128)S(1)}, f32[64,640]{1,0:T(8,128)S(1)}, u32[]{:S(2)}, u32[]{:S(2)}) collective-permute-start(f32[64,640]{1,0:T(8,128)S(1)} %get-tuple-element.89), channel_id=1, source_target_pairs={{30,0},{0,2},{2,4},{4,6},{6,8},{8,10},{10,12},{12,14},{14,16},{16,... | collective-permute-start | bytes 491528 | tf_op jit(solution)/shard_map/while/body/eval_jaxpr/ppermute | solution.py:19
  68.1 6.0 %collective-permute-start.2 = (f32[64,64]{1,0:T(8,128)S(1)}, f32[64,64]{1,0:T(8,128)S(1)}, u32[]{:S(2)}, u32[]{:S(2)}) collective-permute-start(f32[64,64]{1,0:T(8,128)S(1)} %get-tuple-element.94), channel_id=1, source_target_pairs={{30,0},{0,2},{2,4},{4,6},{6,8},{8,10},{10,12},{12,14},{14,16},{16,... | collective-permute-start | bytes 49160 | tf_op jit(solution)/shard_map/while/body/eval_jaxpr/ppermute | solution.py:19
  126.9 6.4 %collective-permute-start.1 = (f32[64,256]{1,0:T(8,128)S(1)}, f32[64,256]{1,0:T(8,128)S(1)}, u32[]{:S(2)}, u32[]{:S(2)}) collective-permute-start(f32[64,256]{1,0:T(8,128)S(1)} %get-tuple-element.91), channel_id=1, source_target_pairs={{30,0},{0,2},{2,4},{4,6},{6,8},{8,10},{10,12},{12,14},{14,16},{16,... | collective-permute-start | bytes 196616 | tf_op jit(solution)/shard_map/while/body/eval_jaxpr/ppermute | solution.py:19
  127.4 7.7 %collective-permute-start = (f32[64,640]{1,0:T(8,128)S(1)}, f32[64,640]{1,0:T(8,128)S(1)}, u32[]{:S(2)}, u32[]{:S(2)}) collective-permute-start(f32[64,640]{1,0:T(8,128)S(1)} %get-tuple-element.89), channel_id=1, source_target_pairs={{30,0},{0,2},{2,4},{4,6},{6,8},{8,10},{10,12},{12,14},{14,16},{16,... | collective-permute-start | bytes 491528 | tf_op jit(solution)/shard_map/while/body/eval_jaxpr/ppermute | solution.py:19
  128.0 7.4 %collective-permute-start.2 = (f32[64,64]{1,0:T(8,128)S(1)}, f32[64,64]{1,0:T(8,128)S(1)}, u32[]{:S(2)}, u32[]{:S(2)}) collective-permute-start(f32[64,64]{1,0:T(8,128)S(1)} %get-tuple-element.94), channel_id=1, source_target_pairs={{30,0},{0,2},{2,4},{4,6},{6,8},{8,10},{10,12},{12,14},{14,16},{16,... | collective-permute-start | bytes 49160 | tf_op jit(solution)/shard_map/while/body/eval_jaxpr/ppermute | solution.py:19
  188.2 6.4 %collective-permute-start.1 = (f32[64,256]{1,0:T(8,128)S(1)}, f32[64,256]{1,0:T(8,128)S(1)}, u32[]{:S(2)}, u32[]{:S(2)}) collective-permute-start(f32[64,256]{1,0:T(8,128)S(1)} %get-tuple-element.91), channel_id=1, source_target_pairs={{30,0},{0,2},{2,4},{4,6},{6,8},{8,10},{10,12},{12,14},{14,16},{16,... | collective-permute-start | bytes 196616 | tf_op jit(solution)/shard_map/while/body/eval_jaxpr/ppermute | solution.py:19
  188.7 7.7 %collective-permute-start = (f32[64,640]{1,0:T(8,128)S(1)}, f32[64,640]{1,0:T(8,128)S(1)}, u32[]{:S(2)}, u32[]{:S(2)}) collective-permute-start(f32[64,640]{1,0:T(8,128)S(1)} %get-tuple-element.89), channel_id=1, source_target_pairs={{30,0},{0,2},{2,4},{4,6},{6,8},{8,10},{10,12},{12,14},{14,16},{16,... | collective-permute-start | bytes 491528 | tf_op jit(solution)/shard_map/while/body/eval_jaxpr/ppermute | solution.py:19
  189.4 7.4 %collective-permute-start.2 = (f32[64,64]{1,0:T(8,128)S(1)}, f32[64,64]{1,0:T(8,128)S(1)}, u32[]{:S(2)}, u32[]{:S(2)}) collective-permute-start(f32[64,64]{1,0:T(8,128)S(1)} %get-tuple-element.94), channel_id=1, source_target_pairs={{30,0},{0,2},{2,4},{4,6},{6,8},{8,10},{10,12},{12,14},{14,16},{16,... | collective-permute-start | bytes 49160 | tf_op jit(solution)/shard_map/while/body/eval_jaxpr/ppermute | solution.py:19
  249.5 6.4 %collective-permute-start.1 = (f32[64,256]{1,0:T(8,128)S(1)}, f32[64,256]{1,0:T(8,128)S(1)}, u32[]{:S(2)}, u32[]{:S(2)}) collective-permute-start(f32[64,256]{1,0:T(8,128)S(1)} %get-tuple-element.91), channel_id=1, source_target_pairs={{30,0},{0,2},{2,4},{4,6},{6,8},{8,10},{10,12},{12,14},{14,16},{16,... | collective-permute-start | bytes 196616 | tf_op jit(solution)/shard_map/while/body/eval_jaxpr/ppermute | solution.py:19
  250.1 7.7 %collective-permute-start = (f32[64,640]{1,0:T(8,128)S(1)}, f32[64,640]{1,0:T(8,128)S(1)}, u32[]{:S(2)}, u32[]{:S(2)}) collective-permute-start(f32[64,640]{1,0:T(8,128)S(1)} %get-tuple-element.89), channel_id=1, source_target_pairs={{30,0},{0,2},{2,4},{4,6},{6,8},{8,10},{10,12},{12,14},{14,16},{16,... | collective-permute-start | bytes 491528 | tf_op jit(solution)/shard_map/while/body/eval_jaxpr/ppermute | solution.py:19
  250.7 7.4 %collective-permute-start.2 = (f32[64,64]{1,0:T(8,128)S(1)}, f32[64,64]{1,0:T(8,128)S(1)}, u32[]{:S(2)}, u32[]{:S(2)}) collective-permute-start(f32[64,64]{1,0:T(8,128)S(1)} %get-tuple-element.94), channel_id=1, source_target_pairs={{30,0},{0,2},{2,4},{4,6},{6,8},{8,10},{10,12},{12,14},{14,16},{16,... | collective-permute-start | bytes 49160 | tf_op jit(solution)/shard_map/while/body/eval_jaxpr/ppermute | solution.py:19
  310.9 6.4 %collective-permute-start.1 = (f32[64,256]{1,0:T(8,128)S(1)}, f32[64,256]{1,0:T(8,128)S(1)}, u32[]{:S(2)}, u32[]{:S(2)}) collective-permute-start(f32[64,256]{1,0:T(8,128)S(1)} %get-tuple-element.91), channel_id=1, source_target_pairs={{30,0},{0,2},{2,4},{4,6},{6,8},{8,10},{10,12},{12,14},{14,16},{16,... | collective-permute-start | bytes 196616 | tf_op jit(solution)/shard_map/while/body/eval_jaxpr/ppermute | solution.py:19
  311.4 7.7 %collective-permute-start = (f32[64,640]{1,0:T(8,128)S(1)}, f32[64,640]{1,0:T(8,128)S(1)}, u32[]{:S(2)}, u32[]{:S(2)}) collective-permute-start(f32[64,640]{1,0:T(8,128)S(1)} %get-tuple-element.89), channel_id=1, source_target_pairs={{30,0},{0,2},{2,4},{4,6},{6,8},{8,10},{10,12},{12,14},{14,16},{16,... | collective-permute-start | bytes 491528 | tf_op jit(solution)/shard_map/while/body/eval_jaxpr/ppermute | solution.py:19
  312.0 7.4 %collective-permute-start.2 = (f32[64,64]{1,0:T(8,128)S(1)}, f32[64,64]{1,0:T(8,128)S(1)}, u32[]{:S(2)}, u32[]{:S(2)}) collective-permute-start(f32[64,64]{1,0:T(8,128)S(1)} %get-tuple-element.94), channel_id=1, source_target_pairs={{30,0},{0,2},{2,4},{4,6},{6,8},{8,10},{10,12},{12,14},{14,16},{16,... | collective-permute-start | bytes 49160 | tf_op jit(solution)/shard_map/while/body/eval_jaxpr/ppermute | solution.py:19
  372.2 6.4 %collective-permute-start.1 = (f32[64,256]{1,0:T(8,128)S(1)}, f32[64,256]{1,0:T(8,128)S(1)}, u32[]{:S(2)}, u32[]{:S(2)}) collective-permute-start(f32[64,256]{1,0:T(8,128)S(1)} %get-tuple-element.91), channel_id=1, source_target_pairs={{30,0},{0,2},{2,4},{4,6},{6,8},{8,10},{10,12},{12,14},{14,16},{16,... | collective-permute-start | bytes 196616 | tf_op jit(solution)/shard_map/while/body/eval_jaxpr/ppermute | solution.py:19
  372.7 7.7 %collective-permute-start = (f32[64,640]{1,0:T(8,128)S(1)}, f32[64,640]{1,0:T(8,128)S(1)}, u32[]{:S(2)}, u32[]{:S(2)}) collective-permute-start(f32[64,640]{1,0:T(8,128)S(1)} %get-tuple-element.89), channel_id=1, source_target_pairs={{30,0},{0,2},{2,4},{4,6},{6,8},{8,10},{10,12},{12,14},{14,16},{16,... | collective-permute-start | bytes 491528 | tf_op jit(solution)/shard_map/while/body/eval_jaxpr/ppermute | solution.py:19
  373.3 7.4 %collective-permute-start.2 = (f32[64,64]{1,0:T(8,128)S(1)}, f32[64,64]{1,0:T(8,128)S(1)}, u32[]{:S(2)}, u32[]{:S(2)}) collective-permute-start(f32[64,64]{1,0:T(8,128)S(1)} %get-tuple-element.94), channel_id=1, source_target_pairs={{30,0},{0,2},{2,4},{4,6},{6,8},{8,10},{10,12},{12,14},{14,16},{16,... | collective-permute-start | bytes 49160 | tf_op jit(solution)/shard_map/while/body/eval_jaxpr/ppermute | solution.py:19
  380.7 0.7 copy-start
  380.7 0.8 copy-start.1
